TPU v7x, 32 devices: a whole 2x2x4 slice. The times are simulated.
32 devices in a mesh: dp: 8 (over y, x, core), tp: 4 (over z).
Axes of the slice: x: 2, y: 2, z: 4, core: 2. Of those that a mesh axis runs over, the one named last changes fastest.
Arguments:
- patches: bfloat16 [16384, 768], P(('dp', 'tp')), may hold values from -6 to 6
- validity: int32 [16, 1024], P('dp'), may hold values from 0 to 1, as said below
- mask_pos: int32 [16, 1024], P('dp'), may hold values 0 or 1
- mask_token: float32 [768], replicated, may hold values from -5 to 5
- ln1_gain: float32 [768], replicated, may hold values from 0.5 to 1.5
- ln1_bias: float32 [768], replicated, may hold values from -3 to 3
- w_qkv: bfloat16 [768, 3, 768], P(None, None, 'tp'), may hold values from -0.21875 to 0.21875
- b_qv: float32 [2, 768], P(None, 'tp'), may hold values from -3 to 3
- w_out: bfloat16 [768, 768], P('tp'), may hold values from -0.625 to 0.625
- b_out: float32 [768], replicated, may hold values from -3 to 3
- ln2_gain: float32 [768], replicated, may hold values from 0.5 to 1.5
- ln2_bias: float32 [768], replicated, may hold values from -3 to 3
- w_up: bfloat16 [768, 3072], P(None, 'tp'), may hold values from -0.21875 to 0.21875
- b_up: float32 [3072], P('tp'), may hold values from -3 to 3
- w_down: bfloat16 [3072, 768], P('tp'), may hold values from -0.109375 to 0.109375
- b_down: float32 [768], replicated, may hold values from -3 to 3
- out_grad: bfloat16 [16384, 768], P(('dp', 'tp')), may hold values from -6 to 6
Outputs:
- output: bfloat16 [16384, 768], P(('dp', 'tp'))
- grad_patches: float32 [16384, 768], P(('dp', 'tp'))
- grad_mask_token: float32 [768], replicated
- grad_ln1_gain: float32 [768], replicated
- grad_ln1_bias: float32 [768], replicated
- grad_w_qkv: float32 [768, 3, 768], P(None, None, 'tp')
- grad_b_qv: float32 [2, 768], P(None, 'tp')
- grad_w_out: float32 [768, 768], P('tp')
- grad_b_out: float32 [768], replicated
- grad_ln2_gain: float32 [768], replicated
- grad_ln2_bias: float32 [768], replicated
- grad_w_up: float32 [768, 3072], P(None, 'tp')
- grad_b_up: float32 [3072], P('tp')
- grad_w_down: float32 [3072, 768], P('tp')
- grad_b_down: float32 [768], replicated
Inputs may be any that keep to these rules, and one draw needn't show every extreme that they name: `validity`: each bucket's valid slots are its first ones, at least 256 of them; buckets whose index is a multiple of 3 are full.
All inputs are finite; a program needn't handle non-finite values. No bound on the sum of `mask_pos` on one device may be relied on, other than what follows from the above.
Results may differ from a plain program's by a relative error of at most 0.017.
Values may be sent and summed in bfloat16 or wider, within the bound.
A program may use at most 128 MiB of HBM per device.

v0:
```python
import jax
import jax.numpy as jnp
from jax import lax
from jax.sharding import PartitionSpec as P

HEAD_DIM = 64


def layer_norm(values, gain, bias):
    center = values - jnp.mean(values, -1, keepdims=True)
    spread = jnp.mean(center * center, -1, keepdims=True)
    return center * lax.rsqrt(spread + 1e-06) * gain + bias


def exact_gelu(values):
    return jax.nn.gelu(values, approximate=False)


def outer_sum(left, right):
    return lax.dot_general(
        left, right, (((0,), (0,)), ((), ())), preferred_element_type=jnp.float32
    )


def dot_trans(left, right):
    return lax.dot_general(
        left, right, (((1,), (1,)), ((), ())), preferred_element_type=jnp.float32
    )


def masked_scores(query_rows, key_rows, keep_key):
    scores = jnp.einsum(
        "qhd,khd->hqk", query_rows, key_rows, preferred_element_type=jnp.float32
    ) * HEAD_DIM ** (-0.5)
    return jnp.where(keep_key[None, None, :] > 0, scores, -1000000000.0)


def attend(bucket_in):
    packed, keep_key = bucket_in
    scores = masked_scores(packed[:, 0], packed[:, 1], keep_key)
    row_max = jnp.max(scores, -1, keepdims=True)
    powered = jnp.exp(scores - row_max)
    row_sum = jnp.sum(powered, -1, keepdims=True)
    weights = (powered / row_sum).astype(jnp.bfloat16)
    context = jnp.einsum("hqk,khd->qhd", weights, packed[:, 2], preferred_element_type=jnp.float32)
    return (context.astype(jnp.bfloat16), (row_max + jnp.log(row_sum))[..., 0])


def attend_back(bucket_in):
    packed, keep_key, log_norm, grad_ctx = bucket_in
    query_rows, key_rows, value_rows = (packed[:, 0], packed[:, 1], packed[:, 2])
    scale_factor = HEAD_DIM ** (-0.5)
    weights = jnp.exp(masked_scores(query_rows, key_rows, keep_key) - log_norm[..., None])
    grad_weights = jnp.einsum(
        "qhd,khd->hqk", grad_ctx, value_rows, preferred_element_type=jnp.float32
    )
    inner = jnp.sum(weights * grad_weights, -1, keepdims=True)
    grad_scores = (weights * (grad_weights - inner)).astype(jnp.bfloat16)
    grad_query = (
        jnp.einsum("hqk,khd->qhd", grad_scores, key_rows, preferred_element_type=jnp.float32)
        * scale_factor
    )
    grad_key = (
        jnp.einsum("hqk,qhd->khd", grad_scores, query_rows, preferred_element_type=jnp.float32)
        * scale_factor
    )
    grad_value = jnp.einsum(
        "hqk,qhd->khd", weights.astype(jnp.bfloat16), grad_ctx, preferred_element_type=jnp.float32
    )
    return jnp.stack([grad_query, grad_key, grad_value], 1).astype(jnp.bfloat16)


def shards(
    patches,
    validity,
    mask_pos,
    mask_token,
    ln1_gain,
    ln1_bias,
    w_qkv,
    b_qv,
    w_out,
    b_out,
    ln2_gain,
    ln2_bias,
    w_up,
    b_up,
    w_down,
    b_down,
    out_grad,
):
    row_count = patches.shape[0]
    model_width = patches.shape[1]
    buckets = validity.shape[0]
    seq_len = validity.shape[1]
    local_width = w_qkv.shape[2]
    local_heads = local_width // HEAD_DIM
    group_rows = buckets * seq_len
    row_start = lax.axis_index("tp") * row_count
    valid_col = lax.dynamic_slice_in_dim(validity.reshape(-1), row_start, row_count).astype(
        jnp.float32
    )[:, None]
    masked_col = lax.dynamic_slice_in_dim(mask_pos.reshape(-1), row_start, row_count).astype(
        jnp.float32
    )[:, None]
    keep_token = valid_col * (1.0 - masked_col)
    swap_token = valid_col * masked_col
    block_in = keep_token * patches.astype(jnp.float32) + swap_token * mask_token[None, :]
    normed_f, ln1_pull = jax.vjp(layer_norm, block_in, ln1_gain, ln1_bias)
    normed_one = normed_f.astype(jnp.bfloat16)
    normed_all = lax.all_gather(normed_one, "tp", axis=0, tiled=True)
    flat_qkv = w_qkv.reshape(model_width, 3 * local_width)
    qkv_rows = jnp.dot(normed_all, flat_qkv, preferred_element_type=jnp.float32).reshape(
        group_rows, 3, local_width
    )
    qkv_bias = jnp.stack([b_qv[0], jnp.zeros_like(b_qv[0]), b_qv[1]])
    qkv_rows = (qkv_rows + qkv_bias[None]).astype(jnp.bfloat16)
    heads_view = qkv_rows.reshape(buckets, seq_len, 3, local_heads, HEAD_DIM)
    context, log_norm = lax.map(attend, (heads_view, validity))
    context = context.reshape(group_rows, local_width)
    attn_part = jnp.dot(context, w_out, preferred_element_type=jnp.float32).astype(jnp.bfloat16)
    attn_rows = lax.psum_scatter(attn_part, "tp", scatter_dimension=0, tiled=True).astype(
        jnp.float32
    )
    residual = block_in + attn_rows + b_out[None, :]
    normed_g, ln2_pull = jax.vjp(layer_norm, residual, ln2_gain, ln2_bias)
    normed_two = normed_g.astype(jnp.bfloat16)
    normed_mlp = lax.all_gather(normed_two, "tp", axis=0, tiled=True)
    hidden_pre = jnp.dot(normed_mlp, w_up, preferred_element_type=jnp.float32) + b_up[None, :]
    gelu_out, gelu_pull = jax.vjp(exact_gelu, hidden_pre)
    hidden = gelu_out.astype(jnp.bfloat16)
    mlp_part = jnp.dot(hidden, w_down, preferred_element_type=jnp.float32).astype(jnp.bfloat16)
    mlp_rows = lax.psum_scatter(mlp_part, "tp", scatter_dimension=0, tiled=True).astype(jnp.float32)
    output = (valid_col * (residual + mlp_rows + b_down[None, :])).astype(jnp.bfloat16)
    grad_out = valid_col * out_grad.astype(jnp.float32)
    grad_b_down = jnp.sum(grad_out, 0)
    grad_out_all = lax.all_gather(grad_out.astype(jnp.bfloat16), "tp", axis=0, tiled=True)
    grad_w_down = outer_sum(hidden, grad_out_all)
    grad_hid = dot_trans(grad_out_all, w_down)
    grad_pre = gelu_pull(grad_hid)[0].astype(jnp.bfloat16)
    grad_w_up = outer_sum(normed_mlp, grad_pre)
    grad_b_up = jnp.sum(grad_pre.astype(jnp.float32), 0)
    grad_normed_two = lax.psum_scatter(
        dot_trans(grad_pre, w_up).astype(jnp.bfloat16), "tp", scatter_dimension=0, tiled=True
    ).astype(jnp.float32)
    grad_res_part, grad_ln2_gain, grad_ln2_bias = ln2_pull(grad_normed_two)
    grad_res = grad_out + grad_res_part
    grad_b_out = jnp.sum(grad_res, 0)
    grad_res_all = lax.all_gather(grad_res.astype(jnp.bfloat16), "tp", axis=0, tiled=True)
    grad_w_out = outer_sum(context, grad_res_all)
    grad_context = dot_trans(grad_res_all, w_out).astype(jnp.bfloat16)
    grad_heads = lax.map(
        attend_back,
        (
            heads_view,
            validity,
            log_norm,
            grad_context.reshape(buckets, seq_len, local_heads, HEAD_DIM),
        ),
    )
    grad_qkv = grad_heads.reshape(group_rows, 3 * local_width)
    grad_w_qkv = outer_sum(normed_all, grad_qkv).reshape(model_width, 3, local_width)
    column_sums = jnp.sum(grad_qkv.astype(jnp.float32), 0).reshape(3, local_width)
    grad_b_qv = jnp.stack([column_sums[0], column_sums[2]])
    grad_normed_one = lax.psum_scatter(
        dot_trans(grad_qkv, flat_qkv).astype(jnp.bfloat16), "tp", scatter_dimension=0, tiled=True
    ).astype(jnp.float32)
    grad_in_part, grad_ln1_gain, grad_ln1_bias = ln1_pull(grad_normed_one)
    grad_in = grad_res + grad_in_part
    grad_patches = keep_token * grad_in
    grad_mask_token = jnp.sum(swap_token * grad_in, 0)
    grad_w_qkv, grad_b_qv, grad_w_out, grad_w_up, grad_b_up, grad_w_down = lax.psum(
        (grad_w_qkv, grad_b_qv, grad_w_out, grad_w_up, grad_b_up, grad_w_down), "dp"
    )
    (
        grad_mask_token,
        grad_ln1_gain,
        grad_ln1_bias,
        grad_b_out,
        grad_ln2_gain,
        grad_ln2_bias,
        grad_b_down,
    ) = lax.psum(
        (
            grad_mask_token,
            grad_ln1_gain,
            grad_ln1_bias,
            grad_b_out,
            grad_ln2_gain,
            grad_ln2_bias,
            grad_b_down,
        ),
        ("dp", "tp"),
    )
    return (
        output,
        grad_patches,
        grad_mask_token,
        grad_ln1_gain,
        grad_ln1_bias,
        grad_w_qkv,
        grad_b_qv,
        grad_w_out,
        grad_b_out,
        grad_ln2_gain,
        grad_ln2_bias,
        grad_w_up,
        grad_b_up,
        grad_w_down,
        grad_b_down,
    )


def solution(mesh):
    return jax.shard_map(
        shards,
        mesh=mesh,
        in_specs=(
            P(("dp", "tp"), None),
            P("dp", None),
            P("dp", None),
            P(),
            P(),
            P(),
            P(None, None, "tp"),
            P(None, "tp"),
            P("tp", None),
            P(),
            P(),
            P(),
            P(None, "tp"),
            P("tp"),
            P("tp", None),
            P(),
            P(("dp", "tp"), None),
        ),
        out_specs=(
            P(("dp", "tp"), None),
            P(("dp", "tp"), None),
            P(),
            P(),
            P(),
            P(None, None, "tp"),
            P(None, "tp"),
            P("tp", None),
            P(),
            P(),
            P(),
            P(None, "tp"),
            P("tp"),
            P("tp", None),
            P(),
        ),
        check_vma=False,
    )
```

profile of v0, /device:TPU:0, one launch (start us, length us, event | category | flops | bytes accessed | tf_op | source)
XLA Modules:
  0.0 791.8 jit_solution(12632221873132776220)
XLA Ops:
  13.2 3.4 add_convert_fusion.3
  17.0 65.9 %all-gather.5.cloned.1.call-done = bf16[2048,768]{1,0:T(8,128)(2,1)} async-done(((bf16[512,768]{1,0:T(8,128)(2,1)}), bf16[2048,768]{1,0:T(8,128)(2,1)}) %all-gather.5.cloned.1.call-update) | async-done | bytes 3145744 | tf_op jit(solution)/shard_map/all_gather | solution.py:111
  83.0 4.1 add_convert_fusion.1
  87.1 2.9 reshape.235
  90.1 2.4 copy.43
  92.5 22.2 %while.22 = (s32[]{:T(128)}, bf16[2,1024,3,64]{1,3,2,0:T(8,128)(2,1)}, f32[2,3,1024]{2,1,0:T(4,128)}, bf16[2,1024,3,3,64]{1,4,3,2,0:T(8,128)(2,1)S(1)}, s32[2,1024]{1,0:T(2,128)}, /*index=5*/s32[]{:T(128)}) while((s32[]{:T(128)}, bf16[2,1024,3,64]{1,3,2,0:T(8,128)(2,1)}, f32[2,3,1024]{2,1,0:T(4,128)}, ...), condition=%wide.region_5.6_spmd, body=%wide.region_2.5_spmd.sunk | while | flops 843249664 | bytes 48296140 | solution.py:119
  93.3 2.4 fusion.107
  95.7 3.2 fusion.108
  98.9 3.2 fusion.109
  106.8 3.2 fusion.108
  110.0 3.2 fusion.109
  114.7 2.6 copy.44
  118.4 2.7 convolution_convert_fusion.3
  121.3 58.9 %reduce-scatter.5.cloned.1.call-done = bf16[512,768]{1,0:T(8,128)(2,1)} async-done(((bf16[2048,768]{1,0:T(8,128)(2,1)}), bf16[512,768]{1,0:T(8,128)(2,1)}) %reduce-scatter.5.cloned.1.call-update) | async-done | bytes 786448 | tf_op jit(solution)/shard_map/reduce_scatter | solution.py:122
  185.4 3.1 add_convert_fusion.2
  190.3 61.6 %all-gather.7.cloned.1.call-done = bf16[2048,768]{1,0:T(8,128)(2,1)} async-done(((bf16[512,768]{1,0:T(8,128)(2,1)}), bf16[2048,768]{1,0:T(8,128)(2,1)}) %all-gather.7.cloned.1.call-update) | async-done | bytes 3145744 | tf_op jit(solution)/shard_map/all_gather | solution.py:128
  251.9 7.5 fusion.69
  259.4 56.6 %all-gather.9.cloned.1.call-done = bf16[2048,768]{1,0:T(8,128)(2,1)} async-done(((bf16[512,768]{1,0:T(8,128)(2,1)}), bf16[2048,768]{1,0:T(8,128)(2,1)}) %all-gather.9.cloned.1.call-update) | async-done | bytes 3145744 | tf_op jit(solution)/shard_map/all_gather | solution.py:137
  316.1 20.2 %convert_reduce_fusion = (f32[768]{0:T(1024)}, bf16[2048,768]{1,0:T(8,128)(2,1)S(1)}, f32[2048,768]{1,0:T(8,128)}) fusion(f32[2048,768]{1,0:T(8,128)} %fusion.69, f32[768]{0:T(1024)} %param.34, bf16[2048,768]{1,0:T(8,128)(2,1)} %all-gather.9.cloned.1.call-done, bf16[768,768]{1,0:T(8,128)(2,1)S(1)} %copy-done), kind=kOutput, calls=%fused_computation.51 | convolution fusion | flops 2533883136 | bytes 20060160 | tf_op jit(solution)/shard_map/dot_general | solution.py:26
  338.0 4.0 convolution_convert_fusion
  342.5 5.7 multiply_convert_fusion.1
  349.9 4.0 convolution_convert_fusion.1
  354.0 47.2 %reduce-scatter.9.cloned.1.call-done = bf16[512,768]{1,0:T(8,128)(2,1)} async-done(((bf16[2048,768]{1,0:T(8,128)(2,1)}), bf16[512,768]{1,0:T(8,128)(2,1)}) %reduce-scatter.9.cloned.1.call-update) | async-done | bytes 786448 | tf_op jit(solution)/shard_map/reduce_scatter | solution.py:143
  401.2 2.8 convert_reduce_fusion.3
  405.9 57.8 %reduce-scatter.7.cloned.1.call-done = bf16[512,768]{1,0:T(8,128)(2,1)} async-done(((bf16[2048,768]{1,0:T(8,128)(2,1)}), bf16[512,768]{1,0:T(8,128)(2,1)}) %reduce-scatter.7.cloned.1.call-update) | async-done | bytes 786448 | tf_op jit(solution)/shard_map/reduce_scatter | solution.py:133
  463.7 4.2 fusion.66
  468.0 63.4 %all-gather.11.cloned.1.call-done = bf16[2048,768]{1,0:T(8,128)(2,1)} async-done(((bf16[512,768]{1,0:T(8,128)(2,1)}), bf16[2048,768]{1,0:T(8,128)(2,1)}) %all-gather.11.cloned.1.call-update) | async-done | bytes 3145744 | tf_op jit(solution)/shard_map/all_gather | solution.py:149
  531.4 3.9 convolution_convert_fusion.4
  535.4 2.7 reshape.237
  539.2 51.5 %while.23 = (s32[]{:T(128)}, bf16[2,1024,3,3,64]{1,4,3,2,0:T(8,128)(2,1)}, bf16[2,1024,3,3,64]{1,4,3,2,0:T(8,128)(2,1)S(1)}, s32[2,1024]{1,0:T(2,128)S(1)}, f32[...) while((s32[]{:T(128)}, bf16[2,1024,3,3,64]{1,4,3,2,0:T(8,128)(2,1)}, ...), condition=%wide.region_15.16_spmd, body=%wide.region_13.15_spmd.sunk | while | flops 2064971776 | bytes 151884048 | solution.py:152
  542.1 4.3 fusion.115
  546.4 4.8 multiply_reduce_fusion.5
  551.2 5.6 multiply_convert_fusion.4
  556.8 4.1 fusion.117
  567.7 4.3 fusion.115
  572.1 4.8 multiply_reduce_fusion.5
  576.8 5.6 multiply_convert_fusion.4
  582.5 4.1 fusion.117
  590.7 4.1 copy.47
  595.9 4.0 convolution_convert_fusion.2
  600.3 7.1 fusion.71
  607.3 4.2 fusion.72
  613.7 3.2 fusion.39
  619.3 14.2 %all-reduce.1 = (f32[2,192]{1,0:T(2,128)}, f32[768]{0:T(1024)}) all-reduce(f32[2,192]{1,0:T(2,128)S(1)} %pad_maximum_fusion.1, f32[768]{0:T(1024)S(1)} %copy-done.58), channel_id=1, replica_groups=mesh['dp'=8,'tp'=4] {'dp'}, use_global_device_ids=true, to_apply=%region_27.28 | all-reduce | flops 1152 | bytes 9216 | tf_op jit(solution)/shard_map/psum | solution.py:172
  633.5 25.6 %reduce-scatter.11.cloned.1.call-done = bf16[512,768]{1,0:T(8,128)(2,1)} async-done(((bf16[2048,768]{1,0:T(8,128)(2,1)}), bf16[512,768]{1,0:T(8,128)(2,1)}) %reduce-scatter.11.cloned.1.call-update) | async-done | bytes 786448 | tf_op jit(solution)/shard_map/reduce_scatter | solution.py:165
  665.1 41.6 %all-reduce = (f32[768]{0:T(1024)}, f32[768]{0:T(1024)}, f32[768]{0:T(1024)}, f32[768]{0:T(1024)}, f32[768]{0:T(1024)}, /*index=5*/f32[768]{0:T(1024)}, f32[768]{0:T(1024)}) all-reduce(f32[768]{0:T(1024)S(1)} %get-tuple-element.105, f32[768]{0:T(1024)S(1)} %get-tuple-element.102, ...), channel_id=1, replica_groups=mesh['dp'=8,'tp'=4] {'dp','tp'}, use_global_device_ids=true, to_apply=%region_20.21 | all-reduce | flops 5376 | bytes 43008 | tf_op jit(solution)/shard_map/psum | solution.py:183
  706.7 70.6 %all-reduce.5.cloned.1.call-done = (f32[768,3,192]{0,2,1:T(8,128)}, f32[192,768]{1,0:T(8,128)}, f32[768,768]{1,0:T(8,128)}, f32[768,768]{1,0:T(8,128)}) async-done(((f32[768,3,192]{0,2,1:T(8,128)}, f32[192,768]{1,0:T(8,128)}, f32[768,768]{1,0:T(8,128)}, f32[768,768]{1,0:T(8,128)}), (f32[768,3,192]{0,2,1:T(8,128)}, f32[192,768]{1,0:T(8,128)}, f32[768,768]{1,0:T(8,128)}, ...) | async-done | bytes 7077904 | tf_op jit(solution)/shard_map/psum | solution.py:172
  777.3 2.9 copy.82
  (223 shorter events, 58.5 us)
Async XLA Ops:
  7.2 308.9 %copy-start = (bf16[768,768]{1,0:T(8,128)(2,1)S(1)}, bf16[768,768]{1,0:T(8,128)(2,1)}, u32[]{:S(2)}) copy-start(bf16[768,768]{1,0:T(8,128)(2,1)} %param.35) | copy-start | bytes 3538948
  7.2 9.8 %copy-start.59 = (f32[2,192]{1,0:T(2,128)S(1)}, f32[2,192]{1,0:T(2,128)}, u32[]{:S(2)}) copy-start(f32[2,192]{1,0:T(2,128)} %param.28) | copy-start | bytes 4612
  7.2 75.8 %all-gather.5.cloned.1.call-start = ((), (), s32[]{:S(2)}) async-start(), calls=%async_computation.4 | async-start | bytes 3932160 | tf_op jit(solution)/shard_map/all_gather | solution.py:111
  8.1 455.6 %copy-start.28 = (f32[512]{0:T(512)}, f32[512]{0:T(512)S(1)}, u32[]{:S(2)}) copy-start(f32[512]{0:T(512)S(1)} %get-tuple-element.151) | copy-start | bytes 6148
  8.8 454.9 %copy-start.30 = (f32[512]{0:T(512)}, f32[512]{0:T(512)S(1)}, u32[]{:S(2)}) copy-start(f32[512]{0:T(512)S(1)} %convert_multiply_fusion.5) | copy-start | bytes 6148
  16.6 163.6 %reduce-scatter.5.cloned.1.call-start = ((), (), s32[]{:S(2)}) async-start(), calls=%async_computation.5 | async-start | bytes 3932160 | tf_op jit(solution)/shard_map/reduce_scatter | solution.py:122
  95.7 3.2 copy-start.23
  106.8 3.2 copy-start.23
  114.7 3.7 copy-start.33
  121.0 59.2 %copy-start.3 = (bf16[512,768]{1,0:T(8,128)(2,1)S(1)}, bf16[512,768]{1,0:T(8,128)(2,1)}, u32[]{:S(2)}) copy-start(bf16[512,768]{1,0:T(8,128)(2,1)} %param.21) | copy-start | bytes 2359300
  121.0 59.2 %copy-start.26 = (f32[768]{0:T(1024)S(1)}, f32[768]{0:T(1024)}, u32[]{:S(2)}) copy-start(f32[768]{0:T(1024)} %param.24) | copy-start | bytes 9220
  121.0 59.2 %copy-start.37 = (f32[768]{0:T(1024)S(1)}, f32[768]{0:T(1024)}, u32[]{:S(2)}) copy-start(f32[768]{0:T(1024)} %param.30) | copy-start | bytes 9220
  121.1 130.9 %all-gather.7.cloned.1.call-start = ((), (), s32[]{:S(2)}) async-start(), calls=%async_computation.6 | async-start | bytes 3932160 | tf_op jit(solution)/shard_map/all_gather | solution.py:128
  180.3 5.1 copy-start.7
  182.2 6.3 copy-start.20
  188.4 127.6 %all-gather.9.cloned.1.call-start = ((), (), s32[]{:S(2)}) async-start(), calls=%async_computation.8 | async-start | bytes 3932160 | tf_op jit(solution)/shard_map/all_gather | solution.py:137
  190.3 210.9 %reduce-scatter.9.cloned.1.call-start = ((), (), s32[]{:S(2)}) async-start(), calls=%async_computation.9 | async-start | bytes 3932160 | tf_op jit(solution)/shard_map/reduce_scatter | solution.py:143
  316.1 21.9 %copy-start.62 = (bf16[768,768]{1,0:T(8,128)(2,1)S(1)}, bf16[768,768]{1,0:T(8,128)(2,1)}, u32[]{:S(2)}) copy-start(bf16[768,768]{1,0:T(8,128)(2,1)} %param.33) | copy-start | bytes 3538948
  342.0 121.7 %reduce-scatter.7.cloned.1.call-start = ((), (), s32[]{:S(2)}) async-start(), calls=%async_computation.7 | async-start | bytes 3932160 | tf_op jit(solution)/shard_map/reduce_scatter | solution.py:133
  353.9 47.3 %copy-start.39 = (f32[512]{0:T(512)S(1)}, f32[512]{0:T(512)}, u32[]{:S(2)}) copy-start(f32[512]{0:T(512)} %copy-done.38) | copy-start | bytes 6148
  353.9 47.3 %copy-start.40 = (f32[768]{0:T(1024)S(1)}, f32[768]{0:T(1024)}, u32[]{:S(2)}) copy-start(f32[768]{0:T(1024)} %param.31) | copy-start | bytes 9220
  353.9 50.1 %copy-start.53 = (f32[512]{0:T(512)S(1)}, f32[512]{0:T(512)}, u32[]{:S(2)}) copy-start(f32[512]{0:T(512)} %copy-done.52) | copy-start | bytes 6148
  353.9 50.1 %copy-start.47 = (f32[512]{0:T(512)S(1)}, f32[512]{0:T(512)}, u32[]{:S(2)}) copy-start(f32[512]{0:T(512)} %copy-done.46) | copy-start | bytes 6148
  353.9 109.8 %copy-start.49 = (f32[512]{0:T(512)S(1)}, f32[512]{0:T(512)}, u32[]{:S(2)}) copy-start(f32[512]{0:T(512)} %copy-done.48) | copy-start | bytes 6148
  354.0 109.8 %copy-start.57 = (f32[768]{0:T(1024)S(1)}, f32[768]{0:T(1024)}, u32[]{:S(2)}) copy-start(f32[768]{0:T(1024)} %param.36) | copy-start | bytes 9220
  354.0 177.5 %all-gather.11.cloned.1.call-start = ((), (), s32[]{:S(2)}) async-start(), calls=%async_computation.10 | async-start | bytes 3932160 | tf_op jit(solution)/shard_map/all_gather | solution.py:149
  405.9 125.5 %copy-start.34 = (bf16[192,768]{1,0:T(8,128)(2,1)S(1)}, bf16[192,768]{1,0:T(8,128)(2,1)}, u32[]{:S(2)}) copy-start(bf16[192,768]{1,0:T(8,128)(2,1)} %param.29) | copy-start | bytes 884740
  467.9 191.3 %reduce-scatter.11.cloned.1.call-start = ((), (), s32[]{:S(2)}) async-start(), calls=%async_computation.11 | async-start | bytes 3932160 | tf_op jit(solution)/shard_map/reduce_scatter | solution.py:165
  535.4 3.8 copy-start.6
  535.4 3.8 copy-start.32
  556.8 4.6 copy-start.2
  582.4 4.6 copy-start.2
  600.0 177.3 %all-reduce.5.cloned.1.call-start = ((), (), s32[]{:S(2)}) async-start(), calls=%async_computation.12 | async-start | bytes 14155776 | tf_op jit(solution)/shard_map/psum | solution.py:172
  600.2 7.1 copy-start.19
  600.3 7.1 copy-start.61
  607.3 4.2 copy-start.9
  607.3 4.2 copy-start.17
  618.6 40.6 %copy-start.4 = (bf16[512,768]{1,0:T(8,128)(2,1)S(1)}, bf16[512,768]{1,0:T(8,128)(2,1)}, u32[]{:S(2)}) copy-start(bf16[512,768]{1,0:T(8,128)(2,1)} %param.21) | copy-start | bytes 2359300
  618.6 40.6 %copy-start.27 = (f32[768]{0:T(1024)S(1)}, f32[768]{0:T(1024)}, u32[]{:S(2)}) copy-start(f32[768]{0:T(1024)} %param.24) | copy-start | bytes 9220
  618.6 40.6 %copy-start.29 = (f32[512]{0:T(512)S(1)}, f32[512]{0:T(512)}, u32[]{:S(2)}) copy-start(f32[512]{0:T(512)} %copy-done.28) | copy-start | bytes 6148
  618.6 40.6 %copy-start.31 = (f32[512]{0:T(512)S(1)}, f32[512]{0:T(512)}, u32[]{:S(2)}) copy-start(f32[512]{0:T(512)} %copy-done.30) | copy-start | bytes 6148
  618.6 40.6 %copy-start.42 = (f32[512]{0:T(512)S(1)}, f32[512]{0:T(512)}, u32[]{:S(2)}) copy-start(f32[512]{0:T(512)} %copy-done.41) | copy-start | bytes 6148
  618.6 40.6 %copy-start.43 = (f32[768]{0:T(1024)S(1)}, f32[768]{0:T(1024)}, u32[]{:S(2)}) copy-start(f32[768]{0:T(1024)} %param.25) | copy-start | bytes 9220
  618.7 40.6 %copy-start.45 = (f32[512]{0:T(512)S(1)}, f32[512]{0:T(512)}, u32[]{:S(2)}) copy-start(f32[512]{0:T(512)} %copy-done.44) | copy-start | bytes 6148
  618.7 42.6 %copy-start.51 = (f32[512]{0:T(512)S(1)}, f32[512]{0:T(512)}, u32[]{:S(2)}) copy-start(f32[512]{0:T(512)} %copy-done.50) | copy-start | bytes 6148
  633.5 29.9 %copy-start.16 = (f32[512,768]{1,0:T(8,128)S(1)}, f32[512,768]{1,0:T(8,128)}, u32[]{:S(2)}) copy-start(f32[512,768]{1,0:T(8,128)} %get-tuple-element.150) | copy-start | bytes 4718596
  777.3 3.8 copy-start.22
  781.1 3.9 copy-start.1
  (35 other events, 57.8 us)
Sparse Core Ops, SparseCore 0:
  16.8 66.1 all-gather.4
  121.2 59.0 reduce-scatter.4
  188.6 63.3 all-gather.6
  253.9 62.0 all-gather.8
  342.1 59.0 reduce-scatter.8
  403.4 60.2 reduce-scatter.6
  468.0 63.3 all-gather.10
  600.1 59.0 reduce-scatter.10
  664.0 113.2 all-reduce.4
where the time goes:
time: 795 us; the launch traced here: 792 us
  waiting for transfers between devices  508 us (64%)
  matrix products  112 us (14%)
  blocking collectives  55.9 us (7%)
  other arithmetic  55.7 us (7%)
  local copies, waits for them, and re-layouts  43.9 us (6%)
  between operations  14.5 us (2%)
    psum x1, waiting for transfers between devices, shards(): lax.psum((grad_w_qkv, grad_b_qv, grad_w_out, grad_w_up, grad_b_up, grad_w...  70.6 us
    all_gather x1, waiting for transfers between devices, shards(): normed_all = lax.all_gather(normed_one, 'tp', axis=0, tiled=True)  65.9 us
    all_gather x1, waiting for transfers between devices, shards(): lax.all_gather(grad_res.astype(jnp.bfloat16), 'tp', axis=0, tiled=True)  63.4 us
    all_gather x1, waiting for transfers between devices, shards(): normed_mlp = lax.all_gather(normed_two, 'tp', axis=0, tiled=True)  61.6 us
    reduce_scatter x1, waiting for transfers between devices, shards(): lax.psum_scatter(attn_part, 'tp', scatter_dimension=0, tiled=True)  58.9 us
    reduce_scatter x1, waiting for transfers between devices, shards(): lax.psum_scatter(mlp_part, 'tp', scatter_dimension=0, tiled=True)  57.8 us
    all_gather x1, waiting for transfers between devices, shards(): lax.all_gather(grad_out.astype(jnp.bfloat16), 'tp', axis=0, tiled=True)  56.6 us
    reduce_scatter x1, waiting for transfers between devices, shards(): lax.psum_scatter(dot_trans(grad_pre, w_up).astype(jnp.bfloat16), 'tp', sc...  47.2 us
  transfers between devices with their start and end apart: 9, of which 9 were waited for; matrix products, arithmetic and copies ran while one was open for 6% of the time, Pallas kernels for 0%

commit v1 on v0

--- a/solution.py
+++ b/solution.py
@@ -108,7 +108,19 @@
     block_in = keep_token * patches.astype(jnp.float32) + swap_token * mask_token[None, :]
     normed_f, ln1_pull = jax.vjp(layer_norm, block_in, ln1_gain, ln1_bias)
     normed_one = normed_f.astype(jnp.bfloat16)
-    normed_all = lax.all_gather(normed_one, "tp", axis=0, tiled=True)
+    current_value, r1 = (lax.axis_size("tp"), lax.axis_index("tp"))
+    normed_all, step_out = (normed_one, 1)
+    while step_out < current_value:
+        column = []
+        idx = 0
+        while idx < current_value:
+            column.append((idx, idx ^ step_out))
+            idx = idx + 1
+        p_next = lax.ppermute(normed_all, "tp", column)
+        r2 = jnp.concatenate([normed_all, p_next], axis=0)
+        block_out = jnp.concatenate([p_next, normed_all], axis=0)
+        normed_all = jnp.where(r1 & step_out == 0, r2, block_out)
+        step_out = 2 * step_out
     flat_qkv = w_qkv.reshape(model_width, 3 * local_width)
     qkv_rows = jnp.dot(normed_all, flat_qkv, preferred_element_type=jnp.float32).reshape(
         group_rows, 3, local_width

time: 795 us -> 826 us (1.039)
  waiting for transfers between devices: 508 us -> 528 us
    ppermute x0 -> x2, waiting for transfers between devices: none -> 85 us  [shards(): p_next = lax.ppermute(normed_all, 'tp', column)]
    all_gather x1 -> x0, waiting for transfers between devices: 65.9 us -> none  [shards(): normed_all = lax.all_gather(normed_one, 'tp', axis=0, tiled=True)]
    unnamed x118 -> x120, local copies, waits for them, and re-layouts: 18.5 us -> 17 us
  transfers between devices with their start and end apart: 9 -> 10, of which waited for: 9 -> 10; matrix products, arithmetic and copies ran while one was open for 6% -> 6% of each run, Pallas kernels for 0% -> 0%
where the time goes in v1:
time: 826 us; the launch traced here: 821 us
  waiting for transfers between devices  528 us (64%)
  matrix products  115 us (14%)
  other arithmetic  56.8 us (7%)
  blocking collectives  56.3 us (7%)
  local copies, waits for them, and re-layouts  42.5 us (5%)
  between operations  14.8 us (2%)
    ppermute x2, waiting for transfers between devices, shards(): p_next = lax.ppermute(normed_all, 'tp', column)  85 us
    psum x1, waiting for transfers between devices, shards(): lax.psum((grad_w_qkv, grad_b_qv, grad_w_out, grad_w_up, grad_b_up, grad_w...  70.6 us
    all_gather x1, waiting for transfers between devices, shards(): lax.all_gather(grad_res.astype(jnp.bfloat16), 'tp', axis=0, tiled=True)  63.4 us
    all_gather x1, waiting for transfers between devices, shards(): normed_mlp = lax.all_gather(normed_two, 'tp', axis=0, tiled=True)  61.6 us
    reduce_scatter x1, waiting for transfers between devices, shards(): lax.psum_scatter(attn_part, 'tp', scatter_dimension=0, tiled=True)  61.3 us
    reduce_scatter x1, waiting for transfers between devices, shards(): lax.psum_scatter(mlp_part, 'tp', scatter_dimension=0, tiled=True)  57.8 us
    all_gather x1, waiting for transfers between devices, shards(): lax.all_gather(grad_out.astype(jnp.bfloat16), 'tp', axis=0, tiled=True)  56.8 us
    reduce_scatter x1, waiting for transfers between devices, shards(): lax.psum_scatter(dot_trans(grad_pre, w_up).astype(jnp.bfloat16), 'tp', sc...  47.2 us
  transfers between devices with their start and end apart: 10, of which 10 were waited for; matrix products, arithmetic and copies ran while one was open for 6% of the time, Pallas kernels for 0%

profile of v1, /device:TPU:0, one launch (start us, length us, event | category | flops | bytes accessed | tf_op | source)
XLA Modules:
  0.0 820.8 jit_solution(14848421062115612660)
XLA Ops:
  14.7 3.1 collective-permute-start
  17.8 17.6 %collective-permute-done = bf16[512,768]{1,0:T(8,128)(2,1)} collective-permute-done((bf16[512,768]{1,0:T(8,128)(2,1)S(1)}, bf16[512,768]{1,0:T(8,128)(2,1)}, u32[]{:S(2)}, u32[]{:S(2)}) %collective-permute-start) | collective-permute-done | bytes 786464 | tf_op jit(solution)/shard_map/ppermute | solution.py:119
  37.4 2.8 collective-permute-start.1
  40.4 67.4 %collective-permute-done.1 = bf16[1024,768]{1,0:T(8,128)(2,1)} collective-permute-done((bf16[1024,768]{1,0:T(8,128)(2,1)S(1)}, bf16[1024,768]{1,0:T(8,128)(2,1)}, u32[]{:S(2)}, u32[]{:S(2)}) %collective-permute-start.1) | collective-permute-done | bytes 1572896 | tf_op jit(solution)/shard_map/ppermute | solution.py:119
  107.7 5.3 add_convert_fusion.1
  113.1 3.1 reshape.235
  118.6 22.2 %while.22 = (s32[]{:T(128)}, bf16[2,1024,3,64]{1,3,2,0:T(8,128)(2,1)}, f32[2,3,1024]{2,1,0:T(4,128)}, bf16[2,1024,3,3,64]{1,4,3,2,0:T(8,128)(2,1)S(1)}, s32[2,1024]{1,0:T(2,128)}, /*index=5*/s32[]{:T(128)}) while((s32[]{:T(128)}, bf16[2,1024,3,64]{1,3,2,0:T(8,128)(2,1)}, f32[2,3,1024]{2,1,0:T(4,128)}, ...), condition=%wide.region_5.6_spmd, body=%wide.region_2.5_spmd.sunk | while | flops 843249664 | bytes 48296140 | solution.py:131
  121.8 3.2 fusion.108
  125.0 3.2 fusion.109
  132.9 3.2 fusion.108
  136.1 3.2 fusion.109
  140.8 2.6 copy.44
  144.5 2.7 convolution_convert_fusion.3
  147.5 61.3 %reduce-scatter.5.cloned.1.call-done = bf16[512,768]{1,0:T(8,128)(2,1)} async-done(((bf16[2048,768]{1,0:T(8,128)(2,1)}), bf16[512,768]{1,0:T(8,128)(2,1)}) %reduce-scatter.5.cloned.1.call-update) | async-done | bytes 786448 | tf_op jit(solution)/shard_map/reduce_scatter | solution.py:134
  213.8 3.1 add_convert_fusion.2
  218.8 61.6 %all-gather.4.cloned.1.call-done = bf16[2048,768]{1,0:T(8,128)(2,1)} async-done(((bf16[512,768]{1,0:T(8,128)(2,1)}), bf16[2048,768]{1,0:T(8,128)(2,1)}) %all-gather.4.cloned.1.call-update) | async-done | bytes 3145744 | tf_op jit(solution)/shard_map/all_gather | solution.py:140
  280.4 7.5 fusion.69
  287.9 56.8 %all-gather.6.cloned.1.call-done = bf16[2048,768]{1,0:T(8,128)(2,1)} async-done(((bf16[512,768]{1,0:T(8,128)(2,1)}), bf16[2048,768]{1,0:T(8,128)(2,1)}) %all-gather.6.cloned.1.call-update) | async-done | bytes 3145744 | tf_op jit(solution)/shard_map/all_gather | solution.py:149
  344.7 20.2 %convert_reduce_fusion = (f32[768]{0:T(1024)}, bf16[2048,768]{1,0:T(8,128)(2,1)S(1)}, f32[2048,768]{1,0:T(8,128)}) fusion(f32[2048,768]{1,0:T(8,128)} %fusion.69, f32[768]{0:T(1024)} %param.34, bf16[2048,768]{1,0:T(8,128)(2,1)} %all-gather.6.cloned.1.call-done, bf16[768,768]{1,0:T(8,128)(2,1)S(1)} %copy-done), kind=kOutput, calls=%fused_computation.51 | convolution fusion | flops 2533883136 | bytes 20060160 | tf_op jit(solution)/shard_map/dot_general | solution.py:26
  366.7 4.1 convolution_convert_fusion
  371.2 5.7 multiply_convert_fusion.1
  378.7 4.0 convolution_convert_fusion.1
  382.8 47.2 %reduce-scatter.9.cloned.1.call-done = bf16[512,768]{1,0:T(8,128)(2,1)} async-done(((bf16[2048,768]{1,0:T(8,128)(2,1)}), bf16[512,768]{1,0:T(8,128)(2,1)}) %reduce-scatter.9.cloned.1.call-update) | async-done | bytes 786448 | tf_op jit(solution)/shard_map/reduce_scatter | solution.py:155
  430.0 2.8 convert_reduce_fusion.3
  434.6 57.8 %reduce-scatter.7.cloned.1.call-done = bf16[512,768]{1,0:T(8,128)(2,1)} async-done(((bf16[2048,768]{1,0:T(8,128)(2,1)}), bf16[512,768]{1,0:T(8,128)(2,1)}) %reduce-scatter.7.cloned.1.call-update) | async-done | bytes 786448 | tf_op jit(solution)/shard_map/reduce_scatter | solution.py:145
  492.5 4.2 fusion.66
  496.7 63.4 %all-gather.8.cloned.1.call-done = bf16[2048,768]{1,0:T(8,128)(2,1)} async-done(((bf16[512,768]{1,0:T(8,128)(2,1)}), bf16[2048,768]{1,0:T(8,128)(2,1)}) %all-gather.8.cloned.1.call-update) | async-done | bytes 3145744 | tf_op jit(solution)/shard_map/all_gather | solution.py:161
  560.2 3.9 convolution_convert_fusion.4
  564.1 2.7 reshape.237
  567.9 51.5 %while.23 = (s32[]{:T(128)}, bf16[2,1024,3,3,64]{1,4,3,2,0:T(8,128)(2,1)}, bf16[2,1024,3,3,64]{1,4,3,2,0:T(8,128)(2,1)S(1)}, s32[2,1024]{1,0:T(2,128)S(1)}, f32[...) while((s32[]{:T(128)}, bf16[2,1024,3,3,64]{1,4,3,2,0:T(8,128)(2,1)}, ...), condition=%wide.region_15.16_spmd, body=%wide.region_13.15_spmd.sunk | while | flops 2064971776 | bytes 151884048 | solution.py:164
  570.8 4.3 fusion.115
  575.1 4.8 multiply_reduce_fusion.5
  579.9 5.6 multiply_convert_fusion.4
  585.5 4.1 fusion.117
  596.5 4.3 fusion.115
  600.8 4.8 multiply_reduce_fusion.5
  605.5 5.6 multiply_convert_fusion.4
  611.2 4.1 fusion.117
  619.4 4.1 copy.47
  624.7 4.0 convolution_convert_fusion.2
  629.0 7.1 fusion.71
  636.1 4.2 fusion.72
  641.9 5.3 fusion.40
  649.5 14.6 %all-reduce.1 = (f32[2,192]{1,0:T(2,128)}, f32[768]{0:T(1024)}) all-reduce(f32[2,192]{1,0:T(2,128)S(1)} %pad_maximum_fusion.1, f32[768]{0:T(1024)S(1)} %copy-done.60), channel_id=1, replica_groups=mesh['dp'=8,'tp'=4] {'dp'}, use_global_device_ids=true, to_apply=%region_27.28 | all-reduce | flops 1152 | bytes 9216 | tf_op jit(solution)/shard_map/psum | solution.py:184
  664.2 23.7 %reduce-scatter.11.cloned.1.call-done = bf16[512,768]{1,0:T(8,128)(2,1)} async-done(((bf16[2048,768]{1,0:T(8,128)(2,1)}), bf16[512,768]{1,0:T(8,128)(2,1)}) %reduce-scatter.11.cloned.1.call-update) | async-done | bytes 786448 | tf_op jit(solution)/shard_map/reduce_scatter | solution.py:177
  693.8 41.7 %all-reduce = (f32[768]{0:T(1024)}, f32[768]{0:T(1024)}, f32[768]{0:T(1024)}, f32[768]{0:T(1024)}, f32[768]{0:T(1024)}, /*index=5*/f32[768]{0:T(1024)}, f32[768]{0:T(1024)}) all-reduce(f32[768]{0:T(1024)S(1)} %get-tuple-element.105, f32[768]{0:T(1024)S(1)} %get-tuple-element.102, ...), channel_id=1, replica_groups=mesh['dp'=8,'tp'=4] {'dp','tp'}, use_global_device_ids=true, to_apply=%region_20.21 | all-reduce | flops 5376 | bytes 43008 | tf_op jit(solution)/shard_map/psum | solution.py:195
  735.4 70.6 %all-reduce.5.cloned.1.call-done = (f32[768,3,192]{0,2,1:T(8,128)}, f32[192,768]{1,0:T(8,128)}, f32[768,768]{1,0:T(8,128)}, f32[768,768]{1,0:T(8,128)}) async-done(((f32[768,3,192]{0,2,1:T(8,128)}, f32[192,768]{1,0:T(8,128)}, f32[768,768]{1,0:T(8,128)}, f32[768,768]{1,0:T(8,128)}), (f32[768,3,192]{0,2,1:T(8,128)}, f32[192,768]{1,0:T(8,128)}, f32[768,768]{1,0:T(8,128)}, ...) | async-done | bytes 7077904 | tf_op jit(solution)/shard_map/psum | solution.py:184
  806.0 2.9 copy.82
  (227 shorter events, 65.9 us)
Async XLA Ops:
  7.2 337.5 %copy-start = (bf16[768,768]{1,0:T(8,128)(2,1)S(1)}, bf16[768,768]{1,0:T(8,128)(2,1)}, u32[]{:S(2)}) copy-start(bf16[768,768]{1,0:T(8,128)(2,1)} %param.35) | copy-start | bytes 3538948
  7.2 201.6 %reduce-scatter.5.cloned.1.call-start = ((), (), s32[]{:S(2)}) async-start(), calls=%async_computation.4 | async-start | bytes 3932160 | tf_op jit(solution)/shard_map/reduce_scatter | solution.py:134
  8.1 484.3 %copy-start.30 = (f32[512]{0:T(512)}, f32[512]{0:T(512)S(1)}, u32[]{:S(2)}) copy-start(f32[512]{0:T(512)S(1)} %get-tuple-element.151) | copy-start | bytes 6148
  8.8 483.7 %copy-start.32 = (f32[512]{0:T(512)}, f32[512]{0:T(512)S(1)}, u32[]{:S(2)}) copy-start(f32[512]{0:T(512)S(1)} %convert_multiply_fusion.5) | copy-start | bytes 6148
  10.4 7.4 copy-start.43
  12.1 5.7 copy-start.52
  12.1 5.7 copy-start.46
  12.1 28.1 %copy-start.61 = (f32[2,192]{1,0:T(2,128)S(1)}, f32[2,192]{1,0:T(2,128)}, u32[]{:S(2)}) copy-start(f32[2,192]{1,0:T(2,128)} %param.28) | copy-start | bytes 4612
  14.7 20.8 %collective-permute-start = (bf16[512,768]{1,0:T(8,128)(2,1)S(1)}, bf16[512,768]{1,0:T(8,128)(2,1)}, u32[]{:S(2)}, u32[]{:S(2)}) collective-permute-start(bf16[512,768]{1,0:T(8,128)(2,1)S(1)} %add_convert_fusion.3), channel_id=1, source_target_pairs={{0,1},{1,0},{2,3},{3,2},{4,5},{5,4},{6,7},{7,6},{8,9},{9,8},{10,11... | collective-permute-start | bytes 2359304 | tf_op jit(solution)/shard_map/ppermute | solution.py:119
  37.4 70.3 %collective-permute-start.1 = (bf16[1024,768]{1,0:T(8,128)(2,1)S(1)}, bf16[1024,768]{1,0:T(8,128)(2,1)}, u32[]{:S(2)}, u32[]{:S(2)}) collective-permute-start(bf16[1024,768]{1,0:T(8,128)(2,1)S(1)} %maximum_select_fusion.1), channel_id=1, source_target_pairs={{0,2},{1,3},{2,0},{3,1},{4,6},{5,7},{6,4},{7,5},{8,10},{9,11},{10,... | collective-permute-start | bytes 4718600 | tf_op jit(solution)/shard_map/ppermute | solution.py:119
  147.2 61.6 %copy-start.3 = (bf16[512,768]{1,0:T(8,128)(2,1)S(1)}, bf16[512,768]{1,0:T(8,128)(2,1)}, u32[]{:S(2)}) copy-start(bf16[512,768]{1,0:T(8,128)(2,1)} %param.21) | copy-start | bytes 2359300
  147.2 61.6 %copy-start.28 = (f32[768]{0:T(1024)S(1)}, f32[768]{0:T(1024)}, u32[]{:S(2)}) copy-start(f32[768]{0:T(1024)} %param.24) | copy-start | bytes 9220
  147.2 61.6 %copy-start.39 = (f32[768]{0:T(1024)S(1)}, f32[768]{0:T(1024)}, u32[]{:S(2)}) copy-start(f32[768]{0:T(1024)} %param.30) | copy-start | bytes 9220
  147.2 133.2 %all-gather.4.cloned.1.call-start = ((), (), s32[]{:S(2)}) async-start(), calls=%async_computation.5 | async-start | bytes 3932160 | tf_op jit(solution)/shard_map/all_gather | solution.py:140
  208.8 5.1 copy-start.7
  210.7 6.3 copy-start.20
  216.9 127.8 %all-gather.6.cloned.1.call-start = ((), (), s32[]{:S(2)}) async-start(), calls=%async_computation.7 | async-start | bytes 3932160 | tf_op jit(solution)/shard_map/all_gather | solution.py:149
  218.8 211.2 %reduce-scatter.9.cloned.1.call-start = ((), (), s32[]{:S(2)}) async-start(), calls=%async_computation.8 | async-start | bytes 3932160 | tf_op jit(solution)/shard_map/reduce_scatter | solution.py:155
  344.7 22.0 %copy-start.63 = (bf16[768,768]{1,0:T(8,128)(2,1)S(1)}, bf16[768,768]{1,0:T(8,128)(2,1)}, u32[]{:S(2)}) copy-start(bf16[768,768]{1,0:T(8,128)(2,1)} %param.33) | copy-start | bytes 3538948
  370.7 121.7 %reduce-scatter.7.cloned.1.call-start = ((), (), s32[]{:S(2)}) async-start(), calls=%async_computation.6 | async-start | bytes 3932160 | tf_op jit(solution)/shard_map/reduce_scatter | solution.py:145
  382.7 47.3 %copy-start.41 = (f32[512]{0:T(512)S(1)}, f32[512]{0:T(512)}, u32[]{:S(2)}) copy-start(f32[512]{0:T(512)} %copy-done.40) | copy-start | bytes 6148
  382.7 47.3 %copy-start.42 = (f32[768]{0:T(1024)S(1)}, f32[768]{0:T(1024)}, u32[]{:S(2)}) copy-start(f32[768]{0:T(1024)} %param.31) | copy-start | bytes 9220
  382.7 50.1 %copy-start.55 = (f32[512]{0:T(512)S(1)}, f32[512]{0:T(512)}, u32[]{:S(2)}) copy-start(f32[512]{0:T(512)} %copy-done.54) | copy-start | bytes 6148
  382.7 50.1 %copy-start.49 = (f32[512]{0:T(512)S(1)}, f32[512]{0:T(512)}, u32[]{:S(2)}) copy-start(f32[512]{0:T(512)} %copy-done.48) | copy-start | bytes 6148
  382.7 109.8 %copy-start.51 = (f32[512]{0:T(512)S(1)}, f32[512]{0:T(512)}, u32[]{:S(2)}) copy-start(f32[512]{0:T(512)} %copy-done.50) | copy-start | bytes 6148
  382.7 109.8 %copy-start.59 = (f32[768]{0:T(1024)S(1)}, f32[768]{0:T(1024)}, u32[]{:S(2)}) copy-start(f32[768]{0:T(1024)} %param.36) | copy-start | bytes 9220
  382.7 177.4 %all-gather.8.cloned.1.call-start = ((), (), s32[]{:S(2)}) async-start(), calls=%async_computation.9 | async-start | bytes 3932160 | tf_op jit(solution)/shard_map/all_gather | solution.py:161
  434.6 125.5 %copy-start.36 = (bf16[192,768]{1,0:T(8,128)(2,1)S(1)}, bf16[192,768]{1,0:T(8,128)(2,1)}, u32[]{:S(2)}) copy-start(bf16[192,768]{1,0:T(8,128)(2,1)} %param.29) | copy-start | bytes 884740
  496.7 191.3 %reduce-scatter.11.cloned.1.call-start = ((), (), s32[]{:S(2)}) async-start(), calls=%async_computation.10 | async-start | bytes 3932160 | tf_op jit(solution)/shard_map/reduce_scatter | solution.py:177
  564.1 3.8 copy-start.6
  564.1 3.8 copy-start.34
  585.5 4.6 copy-start.2
  611.2 4.6 copy-start.2
  628.7 177.3 %all-reduce.5.cloned.1.call-start = ((), (), s32[]{:S(2)}) async-start(), calls=%async_computation.11 | async-start | bytes 14155776 | tf_op jit(solution)/shard_map/psum | solution.py:184
  629.0 7.1 copy-start.19
  629.0 7.1 copy-start.62
  636.1 4.2 copy-start.9
  636.1 4.2 copy-start.17
  648.8 39.1 %copy-start.4 = (bf16[512,768]{1,0:T(8,128)(2,1)S(1)}, bf16[512,768]{1,0:T(8,128)(2,1)}, u32[]{:S(2)}) copy-start(bf16[512,768]{1,0:T(8,128)(2,1)} %param.21) | copy-start | bytes 2359300
  648.8 39.1 %copy-start.29 = (f32[768]{0:T(1024)S(1)}, f32[768]{0:T(1024)}, u32[]{:S(2)}) copy-start(f32[768]{0:T(1024)} %param.24) | copy-start | bytes 9220
  648.9 39.1 %copy-start.31 = (f32[512]{0:T(512)S(1)}, f32[512]{0:T(512)}, u32[]{:S(2)}) copy-start(f32[512]{0:T(512)} %copy-done.30) | copy-start | bytes 6148
  648.9 39.1 %copy-start.33 = (f32[512]{0:T(512)S(1)}, f32[512]{0:T(512)}, u32[]{:S(2)}) copy-start(f32[512]{0:T(512)} %copy-done.32) | copy-start | bytes 6148
  648.9 39.1 %copy-start.44 = (f32[512]{0:T(512)S(1)}, f32[512]{0:T(512)}, u32[]{:S(2)}) copy-start(f32[512]{0:T(512)} %copy-done.43) | copy-start | bytes 6148
  648.9 39.1 %copy-start.45 = (f32[768]{0:T(1024)S(1)}, f32[768]{0:T(1024)}, u32[]{:S(2)}) copy-start(f32[768]{0:T(1024)} %param.25) | copy-start | bytes 9220
  648.9 39.1 %copy-start.47 = (f32[512]{0:T(512)S(1)}, f32[512]{0:T(512)}, u32[]{:S(2)}) copy-start(f32[512]{0:T(512)} %copy-done.46) | copy-start | bytes 6148
  648.9 41.1 %copy-start.53 = (f32[512]{0:T(512)S(1)}, f32[512]{0:T(512)}, u32[]{:S(2)}) copy-start(f32[512]{0:T(512)} %copy-done.52) | copy-start | bytes 6148
  664.2 28.0 %copy-start.16 = (f32[512,768]{1,0:T(8,128)S(1)}, f32[512,768]{1,0:T(8,128)}, u32[]{:S(2)}) copy-start(f32[512,768]{1,0:T(8,128)} %get-tuple-element.150) | copy-start | bytes 4718596
  809.8 3.9 copy-start.1
  (37 other events, 70.8 us)
Sparse Core Ops, SparseCore 0:
  147.3 61.3 reduce-scatter.4
  217.1 63.3 all-gather.3
  282.6 62.0 all-gather.5
  370.9 59.0 reduce-scatter.8
  432.1 60.3 reduce-scatter.6
  496.8 63.3 all-gather.7
  628.8 59.0 reduce-scatter.10
  692.7 113.2 all-reduce.4
